TPU v7x, 256 devices: a whole 4x4x8 slice. The times are simulated.
256 devices in a mesh: dom: 256 (over x, y, z, core).
Axes of the slice: x: 4, y: 4, z: 8, core: 2. Of those that a mesh axis runs over, the one named last changes fastest.
Arguments:
- features: bfloat16 [262144, 512], P('dom'), may hold values from -6 to 6
- embeddings: bfloat16 [262144, 128], P('dom'), may hold values from -6 to 6
- tile_values: bfloat16 [2048, 4, 128, 128], P('dom'), may hold values from -4 to 4
- tile_columns: int32 [2048, 4], P('dom'), may hold values from 0 to 11
- send_blocks: int32 [256, 2, 2], P('dom'), may hold values from 0 to 7
- send_count: int32 [256, 2], P('dom'), may hold values from 1 to 2, as said below
- hub_rows: int32 [512], P('dom'), may hold values from 0 to 1023, as said below
- hub_weight: bfloat16 [262144, 512], P('dom'), may hold values from -4 to 4
- degree: int32 [262144], P('dom'), may hold values from 16 to 64
Outputs:
- hop_features: bfloat16 [3, 262144, 512], P(None, 'dom')
- hop_embeddings: bfloat16 [3, 262144, 128], P(None, 'dom')
Inputs may be any that keep to these rules, and one draw needn't show every extreme that they name: `send_count`: some partition sends 2 blocks to its right and some to its left. `hub_rows`: the 2 hub rows of each partition are distinct local row numbers.
All inputs are finite; a program needn't handle non-finite values.
Results may differ from a plain program's by a relative error of at most 0.012.
Values may be sent and summed in bfloat16 or wider, within the bound.
A program may use at most 64 MiB of HBM per device.

v0:
```python
import jax
import jax.numpy as jnp
from jax import lax
from jax.sharding import Mesh
from jax.sharding import PartitionSpec as P

HOPS = 3
DOM = ("dom_0", "dom_1", "dom_2", "dom_3")


def sent_to_all(array, axis):
    copies = jnp.broadcast_to(array, (lax.axis_size(axis), *array.shape))
    return lax.all_to_all(copies, axis, split_axis=0, concat_axis=0, tiled=True)


def in_order(parts, dim):
    parts = jnp.moveaxis(parts, 0, dim)
    lengths = parts.shape
    return parts.reshape(*lengths[:dim], lengths[dim] * lengths[dim + 1], *lengths[dim + 2 :])


def whole_of(array, axes, dim):
    far, near = axes
    parts = sent_to_all(sent_to_all(array, far), near)
    return in_order(parts.swapaxes(0, 1).reshape(-1, *array.shape), dim)


def shifted(value, axis, steps):
    count = lax.axis_size(axis)
    initial, last = (max(0, -steps), min(count, count - steps))
    return lax.ppermute(value, axis, [(source, source + steps) for source in range(initial, last)])


def body(
    features,
    embeddings,
    tile_values,
    tile_columns,
    send_blocks,
    send_count,
    hub_rows,
    hub_weight,
    degree,
):
    row_count = features.shape[0]
    tile_size = tile_values.shape[2]
    block_count = row_count // tile_size
    send_most = send_blocks.shape[2]
    feature_width = features.shape[1] + embeddings.shape[1]
    rim_rows = send_most * tile_size
    inverse_root = lax.rsqrt(degree.astype(jnp.float32))[:, None]
    current = jnp.concatenate([features, embeddings], axis=1)
    listed = send_blocks[0].reshape(-1)
    live_slots = (jnp.arange(send_most, dtype=jnp.int32)[None, :] < send_count[0][:, None]).reshape(
        -1
    )
    results = []
    for hop_index in range(HOPS):
        scaled = (current.astype(jnp.float32) * inverse_root).astype(jnp.bfloat16)
        blocked = scaled.reshape(block_count, tile_size, feature_width)
        outgoing = blocked[listed]
        outgoing = jnp.where(live_slots[:, None, None], outgoing, jnp.zeros_like(outgoing))
        outgoing = outgoing.reshape(2 * rim_rows, feature_width)
        hub_local = scaled[hub_rows]
        gathered_hubs = whole_of(hub_local, ("dom_0", ("dom_1", "dom_2", "dom_3")), 0)
        hub_sum = jnp.dot(hub_weight, gathered_hubs, preferred_element_type=jnp.float32)
        from_left = shifted(outgoing[rim_rows:], DOM, 1)
        from_right = shifted(outgoing[:rim_rows], DOM, -1)
        extended = jnp.concatenate(
            [
                blocked,
                from_left.reshape(send_most, tile_size, feature_width),
                from_right.reshape(send_most, tile_size, feature_width),
            ],
            axis=0,
        )
        picked = extended[tile_columns]
        local_part = jnp.einsum(
            "bkij,bkjw->biw", tile_values, picked, preferred_element_type=jnp.float32
        )
        summed = local_part.reshape(row_count, feature_width) + hub_sum
        current = (summed * inverse_root).astype(jnp.bfloat16)
        results.append(current)
    stacked = jnp.stack(results)
    split_at = features.shape[1]
    return (stacked[:, :, :split_at], stacked[:, :, split_at:])


def solution(mesh):
    torus = Mesh(mesh.devices.reshape(4, 4, 8, 2), ("dom_0", "dom_1", "dom_2", "dom_3"))
    placed = (
        P(DOM, None),
        P(DOM, None),
        P(DOM, None, None, None),
        P(DOM, None),
        P(DOM, None, None),
        P(DOM, None),
        P(DOM),
        P(DOM, None),
        P(DOM),
    )
    return jax.shard_map(
        body,
        mesh=torus,
        in_specs=placed,
        out_specs=(P(None, DOM, None), P(None, DOM, None)),
        check_vma=False,
    )
```

profile of v0, /device:TPU:2, one launch (start us, length us, event | category | flops | bytes accessed | tf_op | source)
XLA Modules:
  0.0 208.8 jit_solution(6902937056999456313)
XLA Ops:
  2.1 1.8 copy.43
  3.9 2.3 %copy.42 = bf16[1024,512]{0,1:T(8,128)(2,1)} copy(bf16[1024,512]{1,0:T(8,128)(2,1)} %param.9) | data formatting | bytes 2097152 | tf_op args[0]
  6.2 1.7 multiply_convert_fusion.2
  7.9 1.4 copy.44
  9.3 2.0 gather_fusion.2
  12.0 5.5 %all-to-all-start = ((bf16[4,2,640]{2,1,0:T(2,128)(2,1)}), bf16[4,2,640]{2,1,0:T(2,128)(2,1)S(1)}, u32[]{:S(2)}, u32[]{:S(2)}) async-start(bf16[4,2,640]{2,1,0:T(2,128)(2,1)} %broadcast_in_dim.50), calls=%async_computation | async-start | bytes 20480 | tf_op jit(solution)/shard_map/all_to_all | solution.py:13
  19.6 1.7 all-to-all-done
  22.5 11.7 %all-to-all-start.1 = ((bf16[64,4,2,640]{3,2,1,0:T(2,128)(2,1)}), bf16[64,4,2,640]{3,2,1,0:T(2,128)(2,1)}, u32[]{:S(2)}, u32[]{:S(2)}) async-start(bf16[64,4,2,640]{3,2,1,0:T(2,128)(2,1)} %broadcast_in_dim.51), calls=%async_computation.1 | async-start | bytes 1310720 | tf_op jit(solution)/shard_map/all_to_all | solution.py:13
  34.4 7.7 %collective-permute-start.1 = (bf16[256,640]{1,0:T(8,128)(2,1)S(1)}, bf16[256,640]{1,0:T(8,128)(2,1)S(1)}, u32[]{:S(2)}, u32[]{:S(2)}) collective-permute-start(bf16[256,640]{1,0:T(8,128)(2,1)S(1)} %bitcast.98), channel_id=1, source_target_pairs={{1,0},{2,1},{3,2},{4,3},{5,4},{6,5},{7,6},{8,7},{9,8},{10,9},{11,1... | collective-permute-start | bytes 983048 | tf_op jit(solution)/shard_map/ppermute | solution.py:31
  42.1 1.9 collective-permute-start
  44.2 7.6 %collective-permute-done.1 = bf16[256,640]{1,0:T(8,128)(2,1)S(1)} collective-permute-done((bf16[256,640]{1,0:T(8,128)(2,1)S(1)}, bf16[256,640]{1,0:T(8,128)(2,1)S(1)}, u32[]{:S(2)}, u32[]{:S(2)}) %collective-permute-start.1) | collective-permute-done | bytes 327712 | tf_op jit(solution)/shard_map/ppermute | solution.py:31
  51.8 6.6 %collective-permute-done = bf16[256,640]{1,0:T(8,128)(2,1)S(1)} collective-permute-done((bf16[256,640]{1,0:T(8,128)(2,1)S(1)}, bf16[256,640]{1,0:T(8,128)(2,1)S(1)}, u32[]{:S(2)}, u32[]{:S(2)}) %collective-permute-start) | collective-permute-done | bytes 327712 | tf_op jit(solution)/shard_map/ppermute | solution.py:31
  59.2 1.7 pad_maximum_fusion.1
  60.9 3.5 %gather_fusion.1 = bf16[32,128,640]{2,1,0:T(8,128)(2,1)} fusion(bf16[12,128,640]{2,1,0:T(8,128)(2,1)S(1)} %pad_maximum_fusion.1, s32[1024]{0:T(1024)S(1)} %pad_clamp_fusion.1), kind=kCustom, calls=%fused_computation.1 | custom fusion | bytes 10485888 | tf_op jit(solution)/shard_map/gather | solution.py:77
  64.4 5.3 %fusion.12 = f32[8,640,128,1]{1,2,3,0:T(8,128)} fusion(bf16[8,4,128,128]{3,2,1,0:T(8,128)(2,1)} %param.11, bf16[8,4,128,640]{3,2,1,0:T(8,128)(2,1)} %bitcast.82), kind=kOutput, calls=%fused_computation.44 | convolution fusion | flops 671088640 | bytes 8912896 | tf_op jit(solution)/shard_map/bkij,bkjw->biw/dot_general | solution.py:78
  69.7 3.2 %copy.46 = f32[1024,640]{0,1:T(8,128)} copy(f32[1024,640]{1,0:T(8,128)} %bitcast.88) | data formatting | bytes 5242880 | tf_op jit(solution)/shard_map/reshape | solution.py:81
  72.9 1.5 copy.45
  74.7 4.2 %multiply_convert_fusion.1 = (bf16[1024,640]{0,1:T(8,128)(2,1)}, bf16[1024,640]{0,1:T(8,128)(2,1)}) fusion(f32[1024]{0:T(1024)S(1)} %get-tuple-element.14, f32[1024,640]{0,1:T(8,128)} %copy.46, bf16[512,640]{1,0:T(8,128)(2,1)S(1)} %reshape_reshape.9, bf16[1024,512]{1,0:T(8,128)(2,1)S(1)} %copy-done), kind=kOutput, calls=%fused_computation.20 | convolution fusion | flops 675020800 | bytes 6950912 | tf_op jit(solution)/shard_map/dot_general | solution.py:66
  78.9 1.7 copy.64
  81.8 3.9 %all-to-all-start.2 = ((bf16[4,2,640]{2,1,0:T(2,128)(2,1)}), bf16[4,2,640]{2,1,0:T(2,128)(2,1)S(1)}, u32[]{:S(2)}, u32[]{:S(2)}) async-start(bf16[4,2,640]{2,1,0:T(2,128)(2,1)} %broadcast_in_dim.52), calls=%async_computation.2 | async-start | bytes 20480 | tf_op jit(solution)/shard_map/all_to_all | solution.py:13
  86.4 3.2 %all-to-all-done.2 = bf16[4,2,640]{2,1,0:T(2,128)(2,1)S(1)} async-done(((bf16[4,2,640]{2,1,0:T(2,128)(2,1)}), bf16[4,2,640]{2,1,0:T(2,128)(2,1)S(1)}, u32[]{:S(2)}, u32[]{:S(2)}) %all-to-all-start.2) | async-done | bytes 10272 | tf_op jit(solution)/shard_map/all_to_all | solution.py:13
  90.7 5.8 %all-to-all-start.3 = ((bf16[64,4,2,640]{3,2,1,0:T(2,128)(2,1)}), bf16[64,4,2,640]{3,2,1,0:T(2,128)(2,1)}, u32[]{:S(2)}, u32[]{:S(2)}) async-start(bf16[64,4,2,640]{3,2,1,0:T(2,128)(2,1)} %broadcast_in_dim.53), calls=%async_computation.3 | async-start | bytes 1310720 | tf_op jit(solution)/shard_map/all_to_all | solution.py:13
  96.8 7.7 %collective-permute-start.3 = (bf16[256,640]{1,0:T(8,128)(2,1)S(1)}, bf16[256,640]{1,0:T(8,128)(2,1)S(1)}, u32[]{:S(2)}, u32[]{:S(2)}) collective-permute-start(bf16[256,640]{1,0:T(8,128)(2,1)S(1)} %bitcast.101), channel_id=1, source_target_pairs={{1,0},{2,1},{3,2},{4,3},{5,4},{6,5},{7,6},{8,7},{9,8},{10,9},{11,1... | collective-permute-start | bytes 983048 | tf_op jit(solution)/shard_map/ppermute | solution.py:31
  104.4 2.1 %collective-permute-start.2 = (bf16[256,640]{1,0:T(8,128)(2,1)S(1)}, bf16[256,640]{1,0:T(8,128)(2,1)S(1)}, u32[]{:S(2)}, u32[]{:S(2)}) collective-permute-start(bf16[256,640]{1,0:T(8,128)(2,1)S(1)} %bitcast.99), channel_id=1, source_target_pairs={{0,1},{1,2},{2,3},{3,4},{4,5},{5,6},{6,7},{7,8},{8,9},{9,10},{10,1... | collective-permute-start | bytes 983048 | tf_op jit(solution)/shard_map/ppermute | solution.py:31
  106.5 7.6 %collective-permute-done.3 = bf16[256,640]{1,0:T(8,128)(2,1)S(1)} collective-permute-done((bf16[256,640]{1,0:T(8,128)(2,1)S(1)}, bf16[256,640]{1,0:T(8,128)(2,1)S(1)}, u32[]{:S(2)}, u32[]{:S(2)}) %collective-permute-start.3) | collective-permute-done | bytes 327712 | tf_op jit(solution)/shard_map/ppermute | solution.py:31
  114.2 6.6 %collective-permute-done.2 = bf16[256,640]{1,0:T(8,128)(2,1)S(1)} collective-permute-done((bf16[256,640]{1,0:T(8,128)(2,1)S(1)}, bf16[256,640]{1,0:T(8,128)(2,1)S(1)}, u32[]{:S(2)}, u32[]{:S(2)}) %collective-permute-start.2) | collective-permute-done | bytes 327712 | tf_op jit(solution)/shard_map/ppermute | solution.py:31
  120.8 1.6 pad_maximum_fusion.2
  122.4 3.5 %gather_fusion.4 = bf16[32,128,640]{2,1,0:T(8,128)(2,1)} fusion(bf16[12,128,640]{2,1,0:T(8,128)(2,1)S(1)} %pad_maximum_fusion.2, s32[1024]{0:T(1024)S(1)} %pad_clamp_fusion.1), kind=kCustom, calls=%fused_computation.4 | custom fusion | bytes 10485888 | tf_op jit(solution)/shard_map/gather | solution.py:77
  125.9 5.3 %fusion.13 = f32[8,640,128,1]{1,2,3,0:T(8,128)} fusion(bf16[8,4,128,128]{3,2,1,0:T(8,128)(2,1)} %param.11, bf16[8,4,128,640]{3,2,1,0:T(8,128)(2,1)} %bitcast.83), kind=kOutput, calls=%fused_computation.45 | convolution fusion | flops 671088640 | bytes 8912896 | tf_op jit(solution)/shard_map/bkij,bkjw->biw/dot_general | solution.py:78
  131.2 3.2 %copy.62 = f32[1024,640]{0,1:T(8,128)} copy(f32[1024,640]{1,0:T(8,128)} %bitcast.89) | data formatting | bytes 5242880 | tf_op jit(solution)/shard_map/reshape | solution.py:81
  134.4 1.5 copy.51
  136.2 4.2 %multiply_convert_fusion = (bf16[1024,640]{0,1:T(8,128)(2,1)}, bf16[1024,640]{0,1:T(8,128)(2,1)}) fusion(f32[1024]{0:T(1024)S(1)} %get-tuple-element.14, f32[1024,640]{0,1:T(8,128)} %copy.62, bf16[512,640]{1,0:T(8,128)(2,1)S(1)} %reshape_reshape.10, bf16[1024,512]{1,0:T(8,128)(2,1)S(1)} %copy-done), kind=kOutput, calls=%fused_computation.19 | convolution fusion | flops 675020800 | bytes 6950912 | tf_op jit(solution)/shard_map/dot_general | solution.py:66
  140.4 1.7 copy.65
  143.3 3.9 %all-to-all-start.4 = ((bf16[4,2,640]{2,1,0:T(2,128)(2,1)}), bf16[4,2,640]{2,1,0:T(2,128)(2,1)S(1)}, u32[]{:S(2)}, u32[]{:S(2)}) async-start(bf16[4,2,640]{2,1,0:T(2,128)(2,1)} %broadcast_in_dim.54), calls=%async_computation.4 | async-start | bytes 20480 | tf_op jit(solution)/shard_map/all_to_all | solution.py:13
  147.9 3.2 %all-to-all-done.4 = bf16[4,2,640]{2,1,0:T(2,128)(2,1)S(1)} async-done(((bf16[4,2,640]{2,1,0:T(2,128)(2,1)}), bf16[4,2,640]{2,1,0:T(2,128)(2,1)S(1)}, u32[]{:S(2)}, u32[]{:S(2)}) %all-to-all-start.4) | async-done | bytes 10272 | tf_op jit(solution)/shard_map/all_to_all | solution.py:13
  152.2 5.8 %all-to-all-start.5 = ((bf16[64,4,2,640]{3,2,1,0:T(2,128)(2,1)}), bf16[64,4,2,640]{3,2,1,0:T(2,128)(2,1)}, u32[]{:S(2)}, u32[]{:S(2)}) async-start(bf16[64,4,2,640]{3,2,1,0:T(2,128)(2,1)} %broadcast_in_dim.55), calls=%async_computation.5 | async-start | bytes 1310720 | tf_op jit(solution)/shard_map/all_to_all | solution.py:13
  158.3 7.7 %collective-permute-start.5 = (bf16[256,640]{1,0:T(8,128)(2,1)S(1)}, bf16[256,640]{1,0:T(8,128)(2,1)S(1)}, u32[]{:S(2)}, u32[]{:S(2)}) collective-permute-start(bf16[256,640]{1,0:T(8,128)(2,1)S(1)} %bitcast.102), channel_id=1, source_target_pairs={{1,0},{2,1},{3,2},{4,3},{5,4},{6,5},{7,6},{8,7},{9,8},{10,9},{11,1... | collective-permute-start | bytes 983048 | tf_op jit(solution)/shard_map/ppermute | solution.py:31
  165.9 1.9 collective-permute-start.4
  167.9 7.8 %collective-permute-done.5 = bf16[256,640]{1,0:T(8,128)(2,1)S(1)} collective-permute-done((bf16[256,640]{1,0:T(8,128)(2,1)S(1)}, bf16[256,640]{1,0:T(8,128)(2,1)S(1)}, u32[]{:S(2)}, u32[]{:S(2)}) %collective-permute-start.5) | collective-permute-done | bytes 327712 | tf_op jit(solution)/shard_map/ppermute | solution.py:31
  175.7 6.6 %collective-permute-done.4 = bf16[256,640]{1,0:T(8,128)(2,1)S(1)} collective-permute-done((bf16[256,640]{1,0:T(8,128)(2,1)S(1)}, bf16[256,640]{1,0:T(8,128)(2,1)S(1)}, u32[]{:S(2)}, u32[]{:S(2)}) %collective-permute-start.4) | collective-permute-done | bytes 327712 | tf_op jit(solution)/shard_map/ppermute | solution.py:31
  182.3 1.6 pad_maximum_fusion.3
  183.9 3.5 %gather_fusion.7 = bf16[32,128,640]{2,1,0:T(8,128)(2,1)} fusion(bf16[12,128,640]{2,1,0:T(8,128)(2,1)S(1)} %pad_maximum_fusion.3, s32[1024]{0:T(1024)S(1)} %pad_clamp_fusion.1), kind=kCustom, calls=%fused_computation.7 | custom fusion | bytes 10485888 | tf_op jit(solution)/shard_map/gather | solution.py:77
  187.4 5.3 %fusion.14 = f32[8,640,128,1]{1,2,3,0:T(8,128)} fusion(bf16[8,4,128,128]{3,2,1,0:T(8,128)(2,1)} %param.11, bf16[8,4,128,640]{3,2,1,0:T(8,128)(2,1)} %bitcast.81), kind=kOutput, calls=%fused_computation.46 | convolution fusion | flops 671088640 | bytes 8912896 | tf_op jit(solution)/shard_map/bkij,bkjw->biw/dot_general | solution.py:78
  192.7 3.2 %copy.63 = f32[1024,640]{0,1:T(8,128)} copy(f32[1024,640]{1,0:T(8,128)} %bitcast.90) | data formatting | bytes 5242880 | tf_op jit(solution)/shard_map/reshape | solution.py:81
  195.9 1.5 copy.56
  197.8 2.8 %fusion.6 = bf16[1,1024,640]{1,2,0:T(8,128)(2,1)S(1)} fusion(f32[1024,640]{0,1:T(8,128)} %copy.63, bf16[512,640]{1,0:T(8,128)(2,1)S(1)} %reshape_reshape.11, bf16[1024,512]{1,0:T(8,128)(2,1)S(1)} %copy-done, f32[1024]{0:T(1024)S(1)} %get-tuple-element.14), kind=kOutput, calls=%fused_computation.26 | convolution fusion | flops 673054720 | bytes 5640192 | tf_op jit(solution)/shard_map/dot_general | solution.py:66
  201.1 1.9 slice.80
  203.1 4.6 %copy.57 = bf16[3,1024,512]{2,1,0:T(8,128)(2,1)} copy(bf16[3,1024,512]{1,2,0:T(8,128)(2,1)} %slice.80) | data formatting | bytes 6291456
  (61 shorter events, 15.4 us)
Async XLA Ops:
  0.6 74.1 %copy-start = (bf16[1024,512]{1,0:T(8,128)(2,1)S(1)}, bf16[1024,512]{1,0:T(8,128)(2,1)}, u32[]{:S(2)}) copy-start(bf16[1024,512]{1,0:T(8,128)(2,1)} %param.16) | copy-start | bytes 3145732
  6.1 11.3 %copy-start.9 = (s32[1,2,2]{2,1,0:T(2,128)S(1)}, s32[1,2,2]{2,1,0:T(2,128)}, u32[]{:S(2)}) copy-start(s32[1,2,2]{2,1,0:T(2,128)} %param.13) | copy-start | bytes 52
  6.2 11.4 %copy-start.10 = (s32[1,2]{1,0:T(1,128)S(1)}, s32[1,2]{1,0:T(1,128)}, u32[]{:S(2)}) copy-start(s32[1,2]{1,0:T(1,128)} %param.14) | copy-start | bytes 28
  6.2 11.5 %copy-start.6 = (bf16[1024,512]{1,0:T(8,128)(2,1)S(1)}, bf16[1024,512]{1,0:T(8,128)(2,1)}, u32[]{:S(2)}) copy-start(bf16[1024,512]{1,0:T(8,128)(2,1)} %param.9) | copy-start | bytes 3145732
  12.0 9.3 %all-to-all-start = ((bf16[4,2,640]{2,1,0:T(2,128)(2,1)}), bf16[4,2,640]{2,1,0:T(2,128)(2,1)S(1)}, u32[]{:S(2)}, u32[]{:S(2)}) async-start(bf16[4,2,640]{2,1,0:T(2,128)(2,1)} %broadcast_in_dim.50), calls=%async_computation | async-start | bytes 20480 | tf_op jit(solution)/shard_map/all_to_all | solution.py:13
  18.9 15.5 %copy-start.5 = (bf16[8,128,640]{2,1,0:T(8,128)(2,1)}, bf16[8,128,640]{2,1,0:T(8,128)(2,1)S(1)}, u32[]{:S(2)}) copy-start(bf16[8,128,640]{2,1,0:T(8,128)(2,1)S(1)} %multiply_convert_fusion.3) | copy-start | bytes 3932164
  19.6 24.4 %copy-start.8 = (s32[8,4]{0,1:T(4,128)S(1)}, s32[8,4]{0,1:T(4,128)}, u32[]{:S(2)}) copy-start(s32[8,4]{0,1:T(4,128)} %param.12) | copy-start | bytes 388
  22.5 50.4 %all-to-all-start.1 = ((bf16[64,4,2,640]{3,2,1,0:T(2,128)(2,1)}), bf16[64,4,2,640]{3,2,1,0:T(2,128)(2,1)}, u32[]{:S(2)}, u32[]{:S(2)}) async-start(bf16[64,4,2,640]{3,2,1,0:T(2,128)(2,1)} %broadcast_in_dim.51), calls=%async_computation.1 | async-start | bytes 1310720 | tf_op jit(solution)/shard_map/all_to_all | solution.py:13
  34.4 17.4 %collective-permute-start.1 = (bf16[256,640]{1,0:T(8,128)(2,1)S(1)}, bf16[256,640]{1,0:T(8,128)(2,1)S(1)}, u32[]{:S(2)}, u32[]{:S(2)}) collective-permute-start(bf16[256,640]{1,0:T(8,128)(2,1)S(1)} %bitcast.98), channel_id=1, source_target_pairs={{1,0},{2,1},{3,2},{4,3},{5,4},{6,5},{7,6},{8,7},{9,8},{10,9},{11,1... | collective-permute-start | bytes 983048 | tf_op jit(solution)/shard_map/ppermute | solution.py:31
  42.1 16.3 %collective-permute-start = (bf16[256,640]{1,0:T(8,128)(2,1)S(1)}, bf16[256,640]{1,0:T(8,128)(2,1)S(1)}, u32[]{:S(2)}, u32[]{:S(2)}) collective-permute-start(bf16[256,640]{1,0:T(8,128)(2,1)S(1)} %bitcast.97), channel_id=1, source_target_pairs={{0,1},{1,2},{2,3},{3,4},{4,5},{5,6},{6,7},{7,8},{8,9},{9,10},{10,1... | collective-permute-start | bytes 983048 | tf_op jit(solution)/shard_map/ppermute | solution.py:31
  58.4 0.7 copy-start.7
  80.6 16.2 %copy-start.4 = (bf16[1024,640]{1,0:T(8,128)(2,1)}, bf16[1024,640]{1,0:T(8,128)(2,1)S(1)}, u32[]{:S(2)}) copy-start(bf16[1024,640]{1,0:T(8,128)(2,1)S(1)} %copy.64) | copy-start | bytes 3932164
  81.8 7.8 %all-to-all-start.2 = ((bf16[4,2,640]{2,1,0:T(2,128)(2,1)}), bf16[4,2,640]{2,1,0:T(2,128)(2,1)S(1)}, u32[]{:S(2)}, u32[]{:S(2)}) async-start(bf16[4,2,640]{2,1,0:T(2,128)(2,1)} %broadcast_in_dim.52), calls=%async_computation.2 | async-start | bytes 20480 | tf_op jit(solution)/shard_map/all_to_all | solution.py:13
  90.7 43.7 %all-to-all-start.3 = ((bf16[64,4,2,640]{3,2,1,0:T(2,128)(2,1)}), bf16[64,4,2,640]{3,2,1,0:T(2,128)(2,1)}, u32[]{:S(2)}, u32[]{:S(2)}) async-start(bf16[64,4,2,640]{3,2,1,0:T(2,128)(2,1)} %broadcast_in_dim.53), calls=%async_computation.3 | async-start | bytes 1310720 | tf_op jit(solution)/shard_map/all_to_all | solution.py:13
  96.8 17.4 %collective-permute-start.3 = (bf16[256,640]{1,0:T(8,128)(2,1)S(1)}, bf16[256,640]{1,0:T(8,128)(2,1)S(1)}, u32[]{:S(2)}, u32[]{:S(2)}) collective-permute-start(bf16[256,640]{1,0:T(8,128)(2,1)S(1)} %bitcast.101), channel_id=1, source_target_pairs={{1,0},{2,1},{3,2},{4,3},{5,4},{6,5},{7,6},{8,7},{9,8},{10,9},{11,1... | collective-permute-start | bytes 983048 | tf_op jit(solution)/shard_map/ppermute | solution.py:31
  104.4 16.3 %collective-permute-start.2 = (bf16[256,640]{1,0:T(8,128)(2,1)S(1)}, bf16[256,640]{1,0:T(8,128)(2,1)S(1)}, u32[]{:S(2)}, u32[]{:S(2)}) collective-permute-start(bf16[256,640]{1,0:T(8,128)(2,1)S(1)} %bitcast.99), channel_id=1, source_target_pairs={{0,1},{1,2},{2,3},{3,4},{4,5},{5,6},{6,7},{7,8},{8,9},{9,10},{10,1... | collective-permute-start | bytes 983048 | tf_op jit(solution)/shard_map/ppermute | solution.py:31
  142.1 16.2 %copy-start.3 = (bf16[1024,640]{1,0:T(8,128)(2,1)}, bf16[1024,640]{1,0:T(8,128)(2,1)S(1)}, u32[]{:S(2)}) copy-start(bf16[1024,640]{1,0:T(8,128)(2,1)S(1)} %copy.65) | copy-start | bytes 3932164
  143.3 7.8 %all-to-all-start.4 = ((bf16[4,2,640]{2,1,0:T(2,128)(2,1)}), bf16[4,2,640]{2,1,0:T(2,128)(2,1)S(1)}, u32[]{:S(2)}, u32[]{:S(2)}) async-start(bf16[4,2,640]{2,1,0:T(2,128)(2,1)} %broadcast_in_dim.54), calls=%async_computation.4 | async-start | bytes 20480 | tf_op jit(solution)/shard_map/all_to_all | solution.py:13
  152.2 43.7 %all-to-all-start.5 = ((bf16[64,4,2,640]{3,2,1,0:T(2,128)(2,1)}), bf16[64,4,2,640]{3,2,1,0:T(2,128)(2,1)}, u32[]{:S(2)}, u32[]{:S(2)}) async-start(bf16[64,4,2,640]{3,2,1,0:T(2,128)(2,1)} %broadcast_in_dim.55), calls=%async_computation.5 | async-start | bytes 1310720 | tf_op jit(solution)/shard_map/all_to_all | solution.py:13
  158.3 17.4 %collective-permute-start.5 = (bf16[256,640]{1,0:T(8,128)(2,1)S(1)}, bf16[256,640]{1,0:T(8,128)(2,1)S(1)}, u32[]{:S(2)}, u32[]{:S(2)}) collective-permute-start(bf16[256,640]{1,0:T(8,128)(2,1)S(1)} %bitcast.102), channel_id=1, source_target_pairs={{1,0},{2,1},{3,2},{4,3},{5,4},{6,5},{7,6},{8,7},{9,8},{10,9},{11,1... | collective-permute-start | bytes 983048 | tf_op jit(solution)/shard_map/ppermute | solution.py:31
  165.9 16.3 %collective-permute-start.4 = (bf16[256,640]{1,0:T(8,128)(2,1)S(1)}, bf16[256,640]{1,0:T(8,128)(2,1)S(1)}, u32[]{:S(2)}, u32[]{:S(2)}) collective-permute-start(bf16[256,640]{1,0:T(8,128)(2,1)S(1)} %bitcast.100), channel_id=1, source_target_pairs={{0,1},{1,2},{2,3},{3,4},{4,5},{5,6},{6,7},{7,8},{8,9},{9,10},{10,1... | collective-permute-start | bytes 983048 | tf_op jit(solution)/shard_map/ppermute | solution.py:31
  197.7 2.8 %copy-start.1 = (bf16[1024,640]{0,1:T(8,128)(2,1)S(1)}, bf16[1024,640]{0,1:T(8,128)(2,1)}, u32[]{:S(2)}) copy-start(bf16[1024,640]{0,1:T(8,128)(2,1)} %get-tuple-element.17) | copy-start | bytes 3932164
  197.7 2.8 %copy-start.2 = (bf16[1024,640]{0,1:T(8,128)(2,1)S(1)}, bf16[1024,640]{0,1:T(8,128)(2,1)}, u32[]{:S(2)}) copy-start(bf16[1024,640]{0,1:T(8,128)(2,1)} %get-tuple-element.19) | copy-start | bytes 3932164
where the time goes:
time: 210 us; the launch traced here: 209 us
  starting transfers between devices  65.5 us (31%)
  local copies, waits for them, and re-layouts  54.1 us (26%)
  waiting for transfers between devices  51 us (24%)
  matrix products  27 us (13%)
  other arithmetic  10.3 us (5%)
    ppermute x6, waiting for transfers between devices, shifted(): lax.ppermute(value, axis, [(source, source + steps) for source in range(i...  42.9 us
    all_to_all x6, starting transfers between devices, sent_to_all(): return lax.all_to_all(copies, axis, split_axis=0, concat_axis=0, tiled=True)  36.6 us
    ppermute x6, starting transfers between devices, shifted(): lax.ppermute(value, axis, [(source, source + steps) for source in range(i...  28.9 us
    dot_general x3, matrix products, body(): jnp.einsum('bkij,bkjw->biw', tile_values, picked, preferred_element_type=...  15.9 us
    dot_general x3, matrix products, body(): jnp.dot(hub_weight, gathered_hubs, preferred_element_type=jnp.float32)  11.1 us
    unnamed x26, local copies, waits for them, and re-layouts  10.6 us
    gather x3, local copies, waits for them, and re-layouts, body(): picked = extended[tile_columns]  10.6 us
    reshape x3, local copies, waits for them, and re-layouts, body(): summed = local_part.reshape(row_count, feature_width) + hub_sum  9.7 us
  transfers between devices with their start and end apart: 12, of which 9 were waited for; matrix products, arithmetic and copies ran while one was open for 22% of the time, Pallas kernels for 0%

commit v1 on v0

v1 whole, which is shorter than its diff:
```python
import jax
import jax.numpy as jnp
from jax import lax
from jax.experimental import pallas as pl
from jax.experimental.pallas import tpu as pltpu
from jax.sharding import PartitionSpec as P

HOPS = 3
NX, NY, NZ = 4, 4, 8
NG = NX * NY
N_DOM = NG * NZ * 2
HALF_Z = NZ // 2
TILE = 128
ROWS = 1024
BLOCKS = 8
K = 4
F, E = 512, 128
WIDTH = F + E
HUBS = 512
CHUNKS = ((0, 256), (256, 256), (512, 128))
BF16, F32 = jnp.bfloat16, jnp.float32


def kernel(
    feat, emb, tv_hbm, w_hbm, deg, cols, sblk, scnt, hubs,
    outf, oute,
    xf, xe, tv, wv, inv, zs, ext0, ext1, ext2, halo, acc, xo, hsend, land, tsend, gbuf,
    in_sem, hs_sem, hr_sem, s1, r1, s2, r2, s3, r3, out_sem,
):
    exts = (ext0, ext1, ext2)
    me = lax.axis_index("dom")
    core = lax.rem(me, 2)
    z = lax.rem(lax.div(me, 2), NZ)
    g = lax.div(me, 2 * NZ)
    gx = lax.div(g, NY)
    gy = lax.rem(g, NY)
    partner = me + 1 - 2 * core
    cls = lax.div(z, HALF_Z)
    own_slot = lax.rem(z, HALF_Z) * 2 + core

    def dev(g_, z_, c_):
        return (g_ * NZ + z_) * 2 + c_

    def plane(d):
        x_ = lax.rem(gx + lax.div(d, NY), NX)
        y_ = lax.rem(gy + lax.rem(d, NY), NY)
        return x_ * NY + y_

    loads = [
        pltpu.make_async_copy(feat, xf, in_sem.at[0]),
        pltpu.make_async_copy(emb, xe, in_sem.at[1]),
        pltpu.make_async_copy(tv_hbm, tv, in_sem.at[2]),
        pltpu.make_async_copy(w_hbm, wv, in_sem.at[3]),
    ]
    for load in loads:
        load.start()

    barrier = pltpu.get_barrier_semaphore()

    @pl.loop(1, 2 * NZ)
    def _(d):
        pl.semaphore_signal(barrier, inc=1, device_id={"dom": g * 2 * NZ + lax.rem(z * 2 + core + d, 2 * NZ)})

    @pl.loop(1, NG)
    def _(d):
        pl.semaphore_signal(barrier, inc=1, device_id={"dom": dev(plane(d), z, core)})

    @pl.when(me > 0)
    def _():
        pl.semaphore_signal(barrier, inc=1, device_id={"dom": me - 1})

    @pl.when(me < N_DOM - 1)
    def _():
        pl.semaphore_signal(barrier, inc=1, device_id={"dom": me + 1})

    root = lax.rsqrt(deg[...].astype(F32))
    for b in range(BLOCKS):
        inv[b] = jnp.broadcast_to(root[b : b + 1, :], (TILE, TILE)).T

    @pl.when(me == 0)
    def _():
        for h in range(HOPS):
            exts[h][8:10] = jnp.zeros((2, TILE, WIDTH), BF16)

    @pl.when(me == N_DOM - 1)
    def _():
        for h in range(HOPS):
            exts[h][10:12] = jnp.zeros((2, TILE, WIDTH), BF16)

    loads[0].wait()
    loads[1].wait()

    @pl.loop(0, BLOCKS)
    def _(b):
        rows = pl.ds(pl.multiple_of(b * TILE, TILE), TILE)
        scale = inv[b]
        for j in range(F // TILE):
            lanes = slice(j * TILE, (j + 1) * TILE)
            scaled = (xf[rows, lanes].astype(F32) * scale).astype(BF16)
            zs[b, :, lanes] = scaled
            ext0[b, :, lanes] = scaled
        scaled = (xe[rows, :].astype(F32) * scale).astype(BF16)
        zs[b, :, F:] = scaled
        ext0[b, :, F:] = scaled

    def barrier_wait():
        extra = jnp.where(me > 0, 1, 0) + jnp.where(me < N_DOM - 1, 1, 0)
        pl.semaphore_wait(barrier, 2 * NZ - 1 + NG - 1 + extra)

    def first_copy(h, d):
        q = dev(g, lax.rem(z + d, NZ), cls)
        return q, pltpu.make_async_remote_copy(
            src_ref=hsend.at[h], dst_ref=land.at[h, own_slot], send_sem=s1.at[h, d], recv_sem=r1.at[h, own_slot],
            device_id={"dom": q}, device_id_type=pl.DeviceIdType.MESH)

    def second_copy(h, d):
        return pltpu.make_async_remote_copy(
            src_ref=tsend.at[h], dst_ref=gbuf.at[h, g, core], send_sem=s2.at[h, d], recv_sem=r2.at[h, g],
            device_id={"dom": dev(plane(d), z, core)}, device_id_type=pl.DeviceIdType.MESH)

    def arrival(h, d):
        src = plane(d)
        return src, pltpu.make_async_remote_copy(
            src_ref=tsend.at[h], dst_ref=gbuf.at[h, src, core], send_sem=s2.at[h, d], recv_sem=r2.at[h, src],
            device_id={"dom": dev(src, z, core)}, device_id_type=pl.DeviceIdType.MESH)

    def third_copy(h, src, lane):
        return pltpu.make_async_remote_copy(
            src_ref=gbuf.at[h, src, lane], dst_ref=gbuf.at[h, src, lane], send_sem=s3.at[h, src], recv_sem=r3.at[h, src],
            device_id={"dom": partner}, device_id_type=pl.DeviceIdType.MESH)

    def to_left(h):
        return pltpu.make_async_remote_copy(
            src_ref=halo.at[h, 0], dst_ref=exts[h].at[10:12], send_sem=hs_sem.at[h, 0], recv_sem=hr_sem.at[h, 0],
            device_id={"dom": me - 1}, device_id_type=pl.DeviceIdType.MESH)

    def to_right(h):
        return pltpu.make_async_remote_copy(
            src_ref=halo.at[h, 1], dst_ref=exts[h].at[8:10], send_sem=hs_sem.at[h, 1], recv_sem=hr_sem.at[h, 1],
            device_id={"dom": me + 1}, device_id_type=pl.DeviceIdType.MESH)

    for h in range(HOPS):
        picked = []
        for i in range(2):
            r = hubs[i]
            b = lax.shift_right_logical(r, 7)
            rows = zs[b].astype(F32)
            hit = lax.broadcasted_iota(jnp.int32, (TILE, WIDTH), 0) == jnp.bitwise_and(r, TILE - 1)
            picked.append(jnp.sum(jnp.where(hit, rows, 0.0), axis=0, keepdims=True))
        pair = jnp.concatenate(picked, axis=0).astype(BF16)
        hsend[h] = pair
        for j in range(2):
            for s in range(2):
                block = zs[sblk[0, j, s]]
                live = lax.broadcasted_iota(jnp.int32, (TILE, WIDTH), 0) * 0 + s < scnt[0, j]
                halo[h, j, s] = jnp.where(live, block.astype(F32), 0.0).astype(BF16)
        if h == 0:
            barrier_wait()

        @pl.loop(0, NZ)
        def _(d):
            q, copy = first_copy(h, d)

            @pl.when(q != me)
            def _():
                copy.start()

        @pl.when(cls == core)
        def _():
            land[h, own_slot] = pair

        @pl.when(me > 0)
        def _():
            to_left(h).start()

        @pl.when(me < N_DOM - 1)
        def _():
            to_right(h).start()

        for s in range(NZ):
            source = dev(g, core * HALF_Z + s // 2, s % 2)

            @pl.when(source != me)
            def _():
                pltpu.make_async_remote_copy(
                    src_ref=hsend.at[h], dst_ref=land.at[h, s], send_sem=s1.at[h, s], recv_sem=r1.at[h, s],
                    device_id={"dom": source}, device_id_type=pl.DeviceIdType.MESH).wait_recv()

        whole = jnp.concatenate([land[h, s].astype(F32) for s in range(NZ)], axis=0).astype(BF16)
        tsend[h] = whole
        gbuf[h, g, core] = whole

        @pl.loop(1, NG)
        def _(d):
            second_copy(h, d).start()

        third_copy(h, g, core).start()
        if h == 0:
            loads[2].wait()
            loads[3].wait()

        @pl.when(me > 0)
        def _():
            to_right(h).wait_recv()

        @pl.when(me < N_DOM - 1)
        def _():
            to_left(h).wait_recv()

        @pl.loop(0, BLOCKS)
        def _(b):
            left = jnp.concatenate([tv[b, k] for k in range(K)], axis=1)
            right = jnp.concatenate([exts[h][cols[k, b]] for k in range(K)], axis=0)
            acc[b] = jnp.dot(left, right, preferred_element_type=F32)
            for e in range(2):
                d = 2 * b + e

                @pl.when(d > 0)
                def _():
                    src, landed = arrival(h, d)
                    landed.wait_recv()
                    third_copy(h, src, core).start()

        @pl.loop(0, NG)
        def _(src):
            third_copy(h, src, 1 - core).wait_recv()

        for first, count in CHUNKS:
            lanes = slice(first, first + count)
            hub_part = gbuf[h, :, :, :, lanes].reshape(HUBS, count)

            @pl.loop(0, 2)
            def _(half):
                rows = pl.ds(pl.multiple_of(half * 512, 512), 512)
                prod = jnp.dot(wv[rows, :], hub_part, preferred_element_type=F32)
                for q in range(4):
                    b = half * 4 + q
                    scale = inv[b]
                    for j in range(count // TILE):
                        at = slice(first + j * TILE, first + (j + 1) * TILE)
                        y = acc[b, :, at] + prod[q * TILE : (q + 1) * TILE, j * TILE : (j + 1) * TILE]
                        x = (y * scale).astype(BF16)
                        xo[h, pl.ds(pl.multiple_of(b * TILE, TILE), TILE), at] = x
                        if h < HOPS - 1:
                            scaled = (x.astype(F32) * scale).astype(BF16)
                            zs[b, :, at] = scaled
                            exts[h + 1][b, :, at] = scaled

        pltpu.make_async_copy(xo.at[h, :, :F], outf.at[h], out_sem.at[h, 0]).start()
        pltpu.make_async_copy(xo.at[h, :, F:], oute.at[h], out_sem.at[h, 1]).start()

    for h in range(HOPS):
        @pl.loop(0, NZ)
        def _(d):
            q, copy = first_copy(h, d)

            @pl.when(q != me)
            def _():
                copy.wait_send()

        @pl.loop(1, NG)
        def _(d):
            second_copy(h, d).wait_send()

        @pl.loop(0, NG)
        def _(src):
            third_copy(h, src, core).wait_send()

        @pl.when(me > 0)
        def _():
            to_left(h).wait_send()

        @pl.when(me < N_DOM - 1)
        def _():
            to_right(h).wait_send()

        pltpu.make_async_copy(xo.at[h, :, :F], outf.at[h], out_sem.at[h, 0]).wait()
        pltpu.make_async_copy(xo.at[h, :, F:], oute.at[h], out_sem.at[h, 1]).wait()


def body(features, embeddings, tile_values, tile_columns, send_blocks, send_count, hub_rows, hub_weight, degree):
    hbm = pl.BlockSpec(memory_space=pl.ANY)
    vmem = pl.BlockSpec(memory_space=pltpu.VMEM)
    smem = pl.BlockSpec(memory_space=pltpu.SMEM)
    dma = pltpu.SemaphoreType.DMA
    return pl.pallas_call(
        kernel,
        out_shape=(
            jax.ShapeDtypeStruct((HOPS, ROWS, F), BF16),
            jax.ShapeDtypeStruct((HOPS, ROWS, E), BF16),
        ),
        in_specs=[hbm, hbm, hbm, hbm, vmem, smem, smem, smem, smem],
        out_specs=(hbm, hbm),
        scratch_shapes=[
            pltpu.VMEM((ROWS, F), BF16),
            pltpu.VMEM((ROWS, E), BF16),
            pltpu.VMEM((BLOCKS, K, TILE, TILE), BF16),
            pltpu.VMEM((ROWS, HUBS), BF16),
            pltpu.VMEM((BLOCKS, TILE, TILE), F32),
            pltpu.VMEM((BLOCKS, TILE, WIDTH), BF16),
            pltpu.VMEM((12, TILE, WIDTH), BF16),
            pltpu.VMEM((12, TILE, WIDTH), BF16),
            pltpu.VMEM((12, TILE, WIDTH), BF16),
            pltpu.VMEM((HOPS, 2, 2, TILE, WIDTH), BF16),
            pltpu.VMEM((BLOCKS, TILE, WIDTH), F32),
            pltpu.VMEM((HOPS, ROWS, WIDTH), BF16),
            pltpu.VMEM((HOPS, 2, WIDTH), BF16),
            pltpu.VMEM((HOPS, NZ, 2, WIDTH), BF16),
            pltpu.VMEM((HOPS, 16, WIDTH), BF16),
            pltpu.VMEM((HOPS, NG, 2, 16, WIDTH), BF16),
            dma((4,)),
            dma((HOPS, 2)),
            dma((HOPS, 2)),
            dma((HOPS, NZ)),
            dma((HOPS, NZ)),
            dma((HOPS, NG)),
            dma((HOPS, NG)),
            dma((HOPS, NG)),
            dma((HOPS, NG)),
            dma((HOPS, 2)),
        ],
        compiler_params=pltpu.CompilerParams(
            collective_id=0, has_side_effects=True, vmem_limit_bytes=60 * 1024 * 1024
        ),
        name="hops",
    )(features, embeddings, tile_values, hub_weight, degree.reshape(8, 128), tile_columns.T, send_blocks, send_count, hub_rows)


def solution(mesh):
    dom = P("dom", None)
    placed = (dom, dom, P("dom", None, None, None), dom, P("dom", None, None), dom, P("dom"), dom, P("dom"))
    return jax.shard_map(
        body,
        mesh=mesh,
        in_specs=placed,
        out_specs=(P(None, "dom", None), P(None, "dom", None)),
        check_vma=False,
    )
```

time: 210 us -> 68 us (0.32)
  the two profiles are of different devices: /device:TPU:2 before, /device:TPU:3 now
where the time goes in v1:
time: 68 us; the launch traced here: 67.4 us
  Pallas kernels  62 us (91%)
  local copies, waits for them, and re-layouts  4.71 us (7%)
    pallas_call x1, Pallas kernels, body(): pl.pallas_call(kernel, out_shape=(jax.ShapeDtypeStruct((HOPS, ROWS, F), B...  62 us
    unnamed x4, local copies, waits for them, and re-layouts  4.71 us

profile of v1, /device:TPU:3, one launch (start us, length us, event | category | flops | bytes accessed | tf_op | source)
XLA Modules:
  0.0 67.4 jit_solution(10603476690266738791)
XLA Ops:
  0.6 62.0 %hops.1 = (bf16[3,1024,512]{2,1,0:T(8,128)(2,1)}, bf16[3,1024,128]{2,1,0:T(8,128)(2,1)}) custom-call(bf16[1024,512]{1,0:T(8,128)(2,1)} %feat.1, bf16[1024,128]{1,0:T(8,128)(2,1)} %emb.1, bf16[8,4,128,128]{3,2,1,0:T(8,128)(2,1)} %tv_hbm.1, bf16[1024,512]{1,0:T(8,128)(2,1)} %w_hbm.1, s32[8,128]{1,0:T(8,128)} %bitcast.2, s32[4,8]{1,0:T(4,128)} %bitcast.3, ...), custom_call_target="tpu_custom_call" | custom-call | tf_op jit(solution)/shard_map/hops/pallas_call | solution.py:286
  62.7 0.0 copy-start
  62.7 3.8 %copy.13 = bf16[3,1024,512]{2,1,0:T(8,128)(2,1)} copy(bf16[3,1024,512]{2,1,0:T(8,128)(2,1)} %get-tuple-element.4) | data formatting | bytes 6291456
  66.5 0.0 copy-done
  66.5 0.9 %copy.14 = bf16[3,1024,128]{2,1,0:T(8,128)(2,1)} copy(bf16[3,1024,128]{2,1,0:T(8,128)(2,1)S(1)} %copy-done) | data formatting | bytes 1572864
Async XLA Ops:
  62.7 3.8 %copy-start = (bf16[3,1024,128]{2,1,0:T(8,128)(2,1)S(1)}, bf16[3,1024,128]{2,1,0:T(8,128)(2,1)}, u32[]{:S(2)}) copy-start(bf16[3,1024,128]{2,1,0:T(8,128)(2,1)} %get-tuple-element.5) | copy-start | bytes 2359300

commit v2 on v1

v2 whole, which is shorter than its diff:
```python
import jax
import jax.numpy as jnp
from jax import lax
from jax.experimental import pallas as pl
from jax.experimental.pallas import tpu as pltpu
from jax.sharding import PartitionSpec as P

HOPS = 3
NX, NY, NZ = 4, 4, 8
NG = NX * NY
N_DOM = NG * NZ * 2
HALF_Z = NZ // 2
TILE = 128
ROWS = 1024
BLOCKS = 8
K = 4
F, E = 512, 128
WIDTH = F + E
HUBS = 512
CHUNKS = ((0, 256), (256, 256), (512, 128))
LANES = tuple(slice(first, first + count) for first, count in CHUNKS)
FAR_FIRST = (10, 6, 9, 11, 14, 2, 8, 5, 7, 13, 15, 1, 3, 4, 12)
RING_FAR_FIRST = (4, 3, 5, 2, 6, 1, 7, 0)
BF16, F32 = jnp.bfloat16, jnp.float32


def kernel(
    feat, emb, tv_hbm, w_hbm, deg_hbm, cols_hbm, sblk_hbm, scnt_hbm, hubs_hbm,
    xo, wv, inv, acc, gbuf2,
    deg, cols, sblk, scnt, hubs, xf, xe, tv, e00, e01, e02, e10, e11, e12, e20, e21, e22, halo, hsend, land, tsend, gbuf0, gbuf1,
    in_sem, hs_sem, hr_sem, s1, r1, s2, r2, s3, r3,
):
    exts = ((e00, e01, e02), (e10, e11, e12), (e20, e21, e22))
    gbufs = (gbuf0, gbuf1, gbuf2)
    me = lax.axis_index("dom")
    core = lax.rem(me, 2)
    z = lax.rem(lax.div(me, 2), NZ)
    g = lax.div(me, 2 * NZ)
    gx = lax.div(g, NY)
    gy = lax.rem(g, NY)
    partner = me + 1 - 2 * core
    cls = lax.div(z, HALF_Z)
    own_slot = lax.rem(z, HALF_Z) * 2 + core

    def dev(g_, z_, c_):
        return (g_ * NZ + z_) * 2 + c_

    def plane(d):
        x_ = lax.rem(gx + lax.div(d, NY), NX)
        y_ = lax.rem(gy + lax.rem(d, NY), NY)
        return x_ * NY + y_

    def remote(src, dst, send, recv, q):
        return pltpu.make_async_remote_copy(
            src_ref=src, dst_ref=dst, send_sem=send, recv_sem=recv,
            device_id={"dom": q}, device_id_type=pl.DeviceIdType.MESH)

    def first_copy(h, d):
        q = dev(g, lax.rem(z + d, NZ), cls)
        return q, remote(hsend.at[h], land.at[h, own_slot], s1.at[h, d], r1.at[h, own_slot], q)

    def second_copy(h, d):
        return remote(tsend.at[h], gbufs[h].at[g, core], s2.at[h, d], r2.at[h, g], dev(plane(d), z, core))

    def arrival(h, d):
        src = plane(d)
        return src, remote(tsend.at[h], gbufs[h].at[src, core], s2.at[h, d], r2.at[h, src], dev(src, z, core))

    def third_copy(h, src, lane):
        return remote(gbufs[h].at[src, lane], gbufs[h].at[src, lane], s3.at[h, src], r3.at[h, src], partner)

    def to_left(h, n):
        return remote(halo.at[h, 0, :, :, LANES[n]], exts[h][n].at[10:12], hs_sem.at[h, 0, n], hr_sem.at[h, 0, n], me - 1)

    def to_right(h, n):
        return remote(halo.at[h, 1, :, :, LANES[n]], exts[h][n].at[8:10], hs_sem.at[h, 1, n], hr_sem.at[h, 1, n], me + 1)

    small = [
        pltpu.make_async_copy(src, dst, in_sem.at[4 + i])
        for i, (src, dst) in enumerate(
            ((deg_hbm, deg), (cols_hbm, cols), (sblk_hbm, sblk), (scnt_hbm, scnt), (hubs_hbm, hubs)))
    ]
    loads = [
        pltpu.make_async_copy(feat, xf, in_sem.at[0]),
        pltpu.make_async_copy(emb, xe, in_sem.at[1]),
        pltpu.make_async_copy(w_hbm, wv, in_sem.at[2]),
        pltpu.make_async_copy(tv_hbm, tv, in_sem.at[3]),
    ]
    for load in small + loads:
        load.start()

    barrier = pltpu.get_barrier_semaphore()

    @pl.loop(1, 2 * NZ)
    def _(d):
        pl.semaphore_signal(barrier, inc=1, device_id={"dom": g * 2 * NZ + lax.rem(z * 2 + core + d, 2 * NZ)})

    @pl.loop(1, NG)
    def _(d):
        pl.semaphore_signal(barrier, inc=1, device_id={"dom": dev(plane(d), z, core)})

    @pl.when(me > 0)
    def _():
        pl.semaphore_signal(barrier, inc=1, device_id={"dom": me - 1})

    @pl.when(me < N_DOM - 1)
    def _():
        pl.semaphore_signal(barrier, inc=1, device_id={"dom": me + 1})

    def barrier_wait():
        extra = jnp.where(me > 0, 1, 0) + jnp.where(me < N_DOM - 1, 1, 0)
        pl.semaphore_wait(barrier, 2 * NZ - 1 + NG - 1 + extra)

    for load in small:
        load.wait()
    root = lax.rsqrt(deg[...].astype(F32))
    for b in range(BLOCKS):
        inv[b] = jnp.broadcast_to(root[b : b + 1, :], (TILE, TILE)).T

    @pl.when(me == 0)
    def _():
        for h in range(HOPS):
            for n, (_, count) in enumerate(CHUNKS):
                exts[h][n][8:10] = jnp.zeros((2, TILE, count), BF16)

    @pl.when(me == N_DOM - 1)
    def _():
        for h in range(HOPS):
            for n, (_, count) in enumerate(CHUNKS):
                exts[h][n][10:12] = jnp.zeros((2, TILE, count), BF16)

    hub_block = [lax.shift_right_logical(hubs[i], 7) for i in range(2)]
    hub_in = [jnp.bitwise_and(hubs[i], TILE - 1) for i in range(2)]

    def pick(ref):
        rows = []
        for i in range(2):
            block = ref[hub_block[i]].astype(F32)
            hit = lax.broadcasted_iota(jnp.int32, block.shape, 0) == hub_in[i]
            rows.append(jnp.sum(jnp.where(hit, block, 0.0), axis=0, keepdims=True))
        return jnp.concatenate(rows, axis=0)

    def times(block, scale):
        width = block.shape[-1]
        return jnp.concatenate([block[:, j : j + TILE] * scale for j in range(0, width, TILE)], axis=1)

    def send_first(h, pair):
        hsend[h] = pair
        if h == 0:
            barrier_wait()

        for d in RING_FAR_FIRST:
            q, copy = first_copy(h, d)

            @pl.when(q != me)
            def _():
                copy.start()

        @pl.when(cls == core)
        def _():
            land[h, own_slot] = pair

    def listed(j, s, width):
        live = lax.broadcasted_iota(jnp.int32, (TILE, width), 0) * 0 + s < scnt[0, j]
        return sblk[0, j, s], live

    def send_halo(h, n):
        @pl.when(me > 0)
        def _():
            to_left(h, n).start()

        @pl.when(me < N_DOM - 1)
        def _():
            to_right(h, n).start()

    hub_scale = pick(inv)
    loads[0].wait()
    loads[1].wait()
    first = jnp.concatenate([pick(xf), pick(xe)], axis=1)
    send_first(0, times(first, hub_scale).astype(BF16))
    for n, (at, count) in enumerate(CHUNKS):
        for j in range(2):
            for s in range(2):
                b, live = listed(j, s, count)
                block = xf[b, :, LANES[n]] if at < F else xe[b]
                halo[0, j, s, :, LANES[n]] = jnp.where(live, times(block.astype(F32), inv[b]), 0.0).astype(BF16)
        send_halo(0, n)

    @pl.loop(0, BLOCKS)
    def _(b):
        scale = inv[b]
        for n, (at, count) in enumerate(CHUNKS):
            block = xf[b, :, LANES[n]] if at < F else xe[b]
            exts[0][n][b] = times(block.astype(F32), scale).astype(BF16)

    loads[2].wait()
    loads[3].wait()
    hub_w = jnp.concatenate([pick(wv), jnp.zeros((14, HUBS), F32)], axis=0).astype(BF16)

    for h in range(HOPS):
        for s in range(NZ):
            source = dev(g, core * HALF_Z + s // 2, s % 2)

            @pl.when(source != me)
            def _():
                remote(hsend.at[h], land.at[h, s], s1.at[h, s], r1.at[h, s], source).wait_recv()

        whole = jnp.concatenate([land[h, s].astype(F32) for s in range(NZ)], axis=0).astype(BF16)
        tsend[h] = whole
        gbufs[h][g, core] = whole

        for d in FAR_FIRST:
            second_copy(h, d).start()
        third_copy(h, g, core).start()

        for n, (at, count) in enumerate(CHUNKS):
            @pl.when(me > 0)
            def _():
                to_right(h, n).wait_recv()

            @pl.when(me < N_DOM - 1)
            def _():
                to_left(h, n).wait_recv()

            @pl.loop(0, BLOCKS)
            def _(b):
                left = jnp.concatenate([tv[b, k] for k in range(K)], axis=1)
                right = jnp.concatenate([exts[h][n][cols[k, b]] for k in range(K)], axis=0)
                acc[b, :, LANES[n]] = jnp.dot(left, right, preferred_element_type=F32)

        if h < HOPS - 1:
            local_hub = pick(acc)
        for d in FAR_FIRST[::-1]:
            src, landed = arrival(h, d)
            landed.wait_recv()
            third_copy(h, src, core).start()

        @pl.loop(0, NG)
        def _(src):
            third_copy(h, src, 1 - core).wait_recv()

        if h == HOPS - 1:
            break

        gathered = gbufs[h][...].reshape(HUBS, WIDTH)
        y = local_hub + jnp.dot(hub_w, gathered, preferred_element_type=F32)[:2]
        x = times(y, hub_scale).astype(BF16)
        send_first(h + 1, times(x.astype(F32), hub_scale).astype(BF16))

        for n, (at, count) in enumerate(CHUNKS):
            picked = [(j, s, *listed(j, s, count)) for j in range(2) for s in range(2)]
            prod = jnp.dot(
                jnp.concatenate([wv[b] for _, _, b, _ in picked], axis=0),
                gbufs[h][:, :, :, LANES[n]].reshape(HUBS, count), preferred_element_type=F32)
            for i, (j, s, b, live) in enumerate(picked):
                scale = inv[b]
                x = times(acc[b, :, LANES[n]] + prod[i * TILE : (i + 1) * TILE], scale).astype(BF16)
                halo[h + 1, j, s, :, LANES[n]] = jnp.where(live, times(x.astype(F32), scale), 0.0).astype(BF16)
            send_halo(h + 1, n)

        for n, (first, count) in enumerate(CHUNKS):
            hub_part = gbufs[h][:, :, :, LANES[n]].reshape(HUBS, count)

            @pl.loop(0, 2)
            def _(half):
                w_rows = wv[pl.ds(half * 4, 4)].reshape(4 * TILE, HUBS)
                prod = jnp.dot(w_rows, hub_part, preferred_element_type=F32)
                for q in range(4):
                    b = half * 4 + q
                    scale = inv[b]
                    for j in range(count // TILE):
                        at = slice(first + j * TILE, first + (j + 1) * TILE)
                        y = acc[b, :, at] + prod[q * TILE : (q + 1) * TILE, j * TILE : (j + 1) * TILE]
                        x = (y * scale).astype(BF16)
                        xo[h, b, :, at] = x
                        exts[h + 1][n][b, :, j * TILE : (j + 1) * TILE] = (x.astype(F32) * scale).astype(BF16)

    for h in range(HOPS):
        @pl.loop(0, NZ)
        def _(d):
            q, copy = first_copy(h, d)

            @pl.when(q != me)
            def _():
                copy.wait_send()

        @pl.loop(1, NG)
        def _(d):
            second_copy(h, d).wait_send()

        @pl.loop(0, NG)
        def _(src):
            third_copy(h, src, core).wait_send()

        for n in range(len(CHUNKS)):
            @pl.when(me > 0)
            def _():
                to_left(h, n).wait_send()

            @pl.when(me < N_DOM - 1)
            def _():
                to_right(h, n).wait_send()


def last(xo, wv, inv, acc, gbuf, outf, oute, x3, sem):
    def put(h, src, first, count, i):
        if first < F:
            dst = outf.at[h, :, :, first : first + count]
        else:
            dst = oute.at[h]
        return pltpu.make_async_copy(src, dst, sem.at[i])

    puts = [put(h, xo.at[h, :, :, first : first + count], first, count, 2 * h + (first > 0))
            for h in range(HOPS - 1) for first, count in ((0, F), (F, E))]
    for p in puts:
        p.start()
    for n, (first, count) in enumerate(CHUNKS):
        lanes = slice(first, first + count)
        hub_part = gbuf[:, :, :, lanes].reshape(HUBS, count)

        @pl.loop(0, 2)
        def _(half):
            w_rows = wv[pl.ds(half * 4, 4)].reshape(4 * TILE, HUBS)
            prod = jnp.dot(w_rows, hub_part, preferred_element_type=F32)
            for q in range(4):
                b = half * 4 + q
                scale = inv[b]
                for j in range(count // TILE):
                    at = slice(first + j * TILE, first + (j + 1) * TILE)
                    y = acc[b, :, at] + prod[q * TILE : (q + 1) * TILE, j * TILE : (j + 1) * TILE]
                    x3[b, :, at] = (y * scale).astype(BF16)

        p = put(HOPS - 1, x3.at[:, :, lanes], first, count, 4 + n)
        p.start()
        puts.append(p)
    for p in puts:
        p.wait()


def body(features, embeddings, tile_values, tile_columns, send_blocks, send_count, hub_rows, hub_weight, degree):
    hbm = pl.BlockSpec(memory_space=pltpu.HBM)
    vmem = pl.BlockSpec(memory_space=pltpu.VMEM)
    dma = pltpu.SemaphoreType.DMA
    outs = [
        ((HOPS - 1, BLOCKS, TILE, WIDTH), BF16),
        ((BLOCKS, TILE, HUBS), BF16),
        ((BLOCKS, TILE, TILE), F32),
        ((BLOCKS, TILE, WIDTH), F32),
        ((NG, 2, 16, WIDTH), BF16),
    ]
    held = pl.pallas_call(
        kernel,
        out_shape=[pltpu.VMEM(*o) for o in outs],
        in_specs=[hbm] * 9,
        out_specs=[vmem] * 5,
        scratch_shapes=[
            pltpu.VMEM((8, 128), jnp.int32),
            pltpu.SMEM((K, BLOCKS), jnp.int32),
            pltpu.SMEM((1, 2, 2), jnp.int32),
            pltpu.SMEM((1, 2), jnp.int32),
            pltpu.SMEM((2,), jnp.int32),
            pltpu.VMEM((BLOCKS, TILE, F), BF16),
            pltpu.VMEM((BLOCKS, TILE, E), BF16),
            pltpu.VMEM((BLOCKS, K, TILE, TILE), BF16),
            *[pltpu.VMEM((12, TILE, count), BF16) for _ in range(HOPS) for _, count in CHUNKS],
            pltpu.VMEM((HOPS, 2, 2, TILE, WIDTH), BF16),
            pltpu.VMEM((HOPS, 2, WIDTH), BF16),
            pltpu.VMEM((HOPS, NZ, 2, WIDTH), BF16),
            pltpu.VMEM((HOPS, 16, WIDTH), BF16),
            pltpu.VMEM((NG, 2, 16, WIDTH), BF16),
            pltpu.VMEM((NG, 2, 16, WIDTH), BF16),
            dma((9,)),
            dma((HOPS, 2, len(CHUNKS))),
            dma((HOPS, 2, len(CHUNKS))),
            dma((HOPS, NZ)),
            dma((HOPS, NZ)),
            dma((HOPS, NG)),
            dma((HOPS, NG)),
            dma((HOPS, NG)),
            dma((HOPS, NG)),
        ],
        compiler_params=pltpu.CompilerParams(
            collective_id=0, has_side_effects=True, vmem_limit_bytes=59_000_000
        ),
        name="hops",
    )(
        features.reshape(BLOCKS, TILE, F), embeddings.reshape(BLOCKS, TILE, E), tile_values,
        hub_weight.reshape(BLOCKS, TILE, HUBS), degree.reshape(8, 128), tile_columns.T,
        send_blocks, send_count, hub_rows,
    )
    outf, oute = pl.pallas_call(
        last,
        out_shape=(
            jax.ShapeDtypeStruct((HOPS, BLOCKS, TILE, F), BF16),
            jax.ShapeDtypeStruct((HOPS, BLOCKS, TILE, E), BF16),
        ),
        in_specs=[vmem] * 5,
        out_specs=(hbm, hbm),
        scratch_shapes=[pltpu.VMEM((BLOCKS, TILE, WIDTH), BF16), dma((7,))],
        compiler_params=pltpu.CompilerParams(vmem_limit_bytes=16 * 1024 * 1024),
        name="last",
    )(*held)
    return outf.reshape(HOPS, ROWS, F), oute.reshape(HOPS, ROWS, E)


def solution(mesh):
    dom = P("dom", None)
    placed = (dom, dom, P("dom", None, None, None), dom, P("dom", None, None), dom, P("dom"), dom, P("dom"))
    return jax.shard_map(
        body,
        mesh=mesh,
        in_specs=placed,
        out_specs=(P(None, "dom", None), P(None, "dom", None)),
        check_vma=False,
    )
```

time: 68 us -> 56.8 us (0.84)
  Pallas kernels: 62 us -> 56.1 us
  local copies, waits for them, and re-layouts: 4.71 us -> 0 us
    pallas_call x1 -> x2, Pallas kernels: 62 us -> 56.1 us  [the longest x1 53.5 us: body(): pl.pallas_call(kernel, out_shape=[pltpu.VMEM(*o) for o in outs], in_specs...]
    unnamed x4 -> x0, local copies, waits for them, and re-layouts: 4.71 us -> none
where the time goes in v2:
time: 56.8 us; the launch traced here: 56.7 us
  Pallas kernels  56.1 us (99%)
  between operations  0.64 us (1%)
    pallas_call x1, Pallas kernels, body(): pl.pallas_call(kernel, out_shape=[pltpu.VMEM(*o) for o in outs], in_specs...  53.5 us
    pallas_call x1, Pallas kernels, body(): pl.pallas_call(last, out_shape=(jax.ShapeDtypeStruct((HOPS, BLOCKS, TILE,...  2.62 us

profile of v2, /device:TPU:3, one launch (start us, length us, event | category | flops | bytes accessed | tf_op | source)
XLA Modules:
  0.0 56.7 jit_solution(16389307180262860897)
XLA Ops:
  0.6 53.5 %hops.1 = (bf16[2,8,128,640]{3,2,1,0:T(8,128)(2,1)S(1)}, bf16[8,128,512]{2,1,0:T(8,128)(2,1)S(1)}, f32[8,128,128]{2,1,0:T(8,128)S(1)}, f32[8,128,640]{2,1,0:T(8,128)S(1)}, bf16[16,2,16,640]{3,2,1,0:T(8,128)(2,1)S(1)}) custom-call(bf16[8,128,512]{2,1,0:T(8,128)(2,1)} %bitcast.7, bf16[8,128,128]{2,1,0:T(8,128)(2,1)} %bitcast.9, ...), custom_call_target="tpu_custom_call" | custom-call | tf_op jit(solution)/shard_map/hops/pallas_call | solution.py:351
  54.1 2.6 %last.1 = (bf16[3,8,128,512]{3,2,1,0:T(8,128)(2,1)}, bf16[3,8,128,128]{3,2,1,0:T(8,128)(2,1)}) custom-call(bf16[2,8,128,640]{3,2,1,0:T(8,128)(2,1)S(1)} %get-tuple-element.9.xo, bf16[8,128,512]{2,1,0:T(8,128)(2,1)S(1)} %get-tuple-element.10.wv, f32[8,128,128]{2,1,0:T(8,128)S(1)} %get-tuple-element.11.inv, f32[8,128,640]{2,1,0:T(8,128)S(1)} %get-tuple-element.12.acc, ...), custom_call_target="tpu_custom_call" | custom-call | tf_op jit(solution)/shard_map/last/pallas_call | solution.py:391

commit v3 on v2

--- a/solution.py
+++ b/solution.py
@@ -222,7 +222,7 @@
             def _():
                 to_left(h, n).wait_recv()
 
-            @pl.loop(0, BLOCKS)
+            @pl.loop(0, BLOCKS, unroll=8)
             def _(b):
                 left = jnp.concatenate([tv[b, k] for k in range(K)], axis=1)
                 right = jnp.concatenate([exts[h][n][cols[k, b]] for k in range(K)], axis=0)
@@ -261,7 +261,7 @@
         for n, (first, count) in enumerate(CHUNKS):
             hub_part = gbufs[h][:, :, :, LANES[n]].reshape(HUBS, count)
 
-            @pl.loop(0, 2)
+            @pl.loop(0, 2, unroll=2)
             def _(half):
                 w_rows = wv[pl.ds(half * 4, 4)].reshape(4 * TILE, HUBS)
                 prod = jnp.dot(w_rows, hub_part, preferred_element_type=F32)

time: 56.8 us -> 55.2 us (0.972)
  Pallas kernels: 56.1 us -> 54.5 us
    pallas_call x1, Pallas kernels: 53.5 us -> 51.9 us  [body(): pl.pallas_call(kernel, out_shape=[pltpu.VMEM(*o) for o in outs], in_specs...]
where the time goes in v3:
time: 55.2 us; the launch traced here: 55.1 us
  Pallas kernels  54.5 us (99%)
  between operations  0.64 us (1%)
    pallas_call x1, Pallas kernels, body(): pl.pallas_call(kernel, out_shape=[pltpu.VMEM(*o) for o in outs], in_specs...  51.9 us
    pallas_call x1, Pallas kernels, body(): pl.pallas_call(last, out_shape=(jax.ShapeDtypeStruct((HOPS, BLOCKS, TILE,...  2.62 us

profile of v3, /device:TPU:3, one launch (start us, length us, event | category | flops | bytes accessed | tf_op | source)
XLA Modules:
  0.0 55.1 jit_solution(17697758982243720269)
XLA Ops:
  0.6 51.9 %hops.1 = (bf16[2,8,128,640]{3,2,1,0:T(8,128)(2,1)S(1)}, bf16[8,128,512]{2,1,0:T(8,128)(2,1)S(1)}, f32[8,128,128]{2,1,0:T(8,128)S(1)}, f32[8,128,640]{2,1,0:T(8,128)S(1)}, bf16[16,2,16,640]{3,2,1,0:T(8,128)(2,1)S(1)}) custom-call(bf16[8,128,512]{2,1,0:T(8,128)(2,1)} %bitcast.7, bf16[8,128,128]{2,1,0:T(8,128)(2,1)} %bitcast.9, ...), custom_call_target="tpu_custom_call" | custom-call | tf_op jit(solution)/shard_map/hops/pallas_call | solution.py:351
  52.5 2.6 %last.1 = (bf16[3,8,128,512]{3,2,1,0:T(8,128)(2,1)}, bf16[3,8,128,128]{3,2,1,0:T(8,128)(2,1)}) custom-call(bf16[2,8,128,640]{3,2,1,0:T(8,128)(2,1)S(1)} %get-tuple-element.9.xo, bf16[8,128,512]{2,1,0:T(8,128)(2,1)S(1)} %get-tuple-element.10.wv, f32[8,128,128]{2,1,0:T(8,128)S(1)} %get-tuple-element.11.inv, f32[8,128,640]{2,1,0:T(8,128)S(1)} %get-tuple-element.12.acc, ...), custom_call_target="tpu_custom_call" | custom-call | tf_op jit(solution)/shard_map/last/pallas_call | solution.py:391

commit v4 on v3

--- a/solution.py
+++ b/solution.py
@@ -50,6 +50,12 @@
         y_ = lax.rem(gy + lax.rem(d, NY), NY)
         return x_ * NY + y_
 
+    def target(d):
+        way = 1 - 2 * core
+        x_ = lax.rem(gx + NX + way * (d // NY), NX)
+        y_ = lax.rem(gy + NY + way * (d % NY), NY)
+        return x_ * NY + y_
+
     def remote(src, dst, send, recv, q):
         return pltpu.make_async_remote_copy(
             src_ref=src, dst_ref=dst, send_sem=send, recv_sem=recv,
@@ -60,7 +66,7 @@
         return q, remote(hsend.at[h], land.at[h, own_slot], s1.at[h, d], r1.at[h, own_slot], q)
 
     def second_copy(h, d):
-        return remote(tsend.at[h], gbufs[h].at[g, core], s2.at[h, d], r2.at[h, g], dev(plane(d), z, core))
+        return remote(tsend.at[h], gbufs[h].at[g, core], s2.at[h, d], r2.at[h, g], dev(target(d), z, core))
 
     def arrival(h, d):
         src = plane(d)
@@ -86,9 +92,6 @@
         pltpu.make_async_copy(w_hbm, wv, in_sem.at[2]),
         pltpu.make_async_copy(tv_hbm, tv, in_sem.at[3]),
     ]
-    for load in small + loads:
-        load.start()
-
     barrier = pltpu.get_barrier_semaphore()
 
     @pl.loop(1, 2 * NZ)
@@ -106,6 +109,9 @@
     @pl.when(me < N_DOM - 1)
     def _():
         pl.semaphore_signal(barrier, inc=1, device_id={"dom": me + 1})
+
+    for load in small + loads:
+        load.start()
 
     def barrier_wait():
         extra = jnp.where(me > 0, 1, 0) + jnp.where(me < N_DOM - 1, 1, 0)
@@ -284,8 +290,7 @@
             def _():
                 copy.wait_send()
 
-        @pl.loop(1, NG)
-        def _(d):
+        for d in range(1, NG):
             second_copy(h, d).wait_send()
 
         @pl.loop(0, NG)
@@ -318,7 +323,7 @@
         lanes = slice(first, first + count)
         hub_part = gbuf[:, :, :, lanes].reshape(HUBS, count)
 
-        @pl.loop(0, 2)
+        @pl.loop(0, 2, unroll=2)
         def _(half):
             w_rows = wv[pl.ds(half * 4, 4)].reshape(4 * TILE, HUBS)
             prod = jnp.dot(w_rows, hub_part, preferred_element_type=F32)

time: 55.2 us -> 54.1 us (0.980)
  Pallas kernels: 54.5 us -> 53.3 us
    pallas_call x1, Pallas kernels: 2.62 us -> 1.99 us  [body(): pl.pallas_call(last, out_shape=(jax.ShapeDtypeStruct((HOPS, BLOCKS, TILE,...]
where the time goes in v4:
time: 54.1 us; the launch traced here: 54 us
  Pallas kernels  53.3 us (99%)
  between operations  0.64 us (1%)
    pallas_call x1, Pallas kernels, body(): pl.pallas_call(kernel, out_shape=[pltpu.VMEM(*o) for o in outs], in_specs...  51.3 us
    pallas_call x1, Pallas kernels, body(): pl.pallas_call(last, out_shape=(jax.ShapeDtypeStruct((HOPS, BLOCKS, TILE,...  1.99 us

profile of v4, /device:TPU:3, one launch (start us, length us, event | category | flops | bytes accessed | tf_op | source)
XLA Modules:
  0.0 54.0 jit_solution(9291771780851362994)
XLA Ops:
  0.6 51.3 %hops.1 = (bf16[2,8,128,640]{3,2,1,0:T(8,128)(2,1)S(1)}, bf16[8,128,512]{2,1,0:T(8,128)(2,1)S(1)}, f32[8,128,128]{2,1,0:T(8,128)S(1)}, f32[8,128,640]{2,1,0:T(8,128)S(1)}, bf16[16,2,16,640]{3,2,1,0:T(8,128)(2,1)S(1)}) custom-call(bf16[8,128,512]{2,1,0:T(8,128)(2,1)} %bitcast.7, bf16[8,128,128]{2,1,0:T(8,128)(2,1)} %bitcast.9, ...), custom_call_target="tpu_custom_call" | custom-call | tf_op jit(solution)/shard_map/hops/pallas_call | solution.py:356
  52.0 2.0 %last.1 = (bf16[3,8,128,512]{3,2,1,0:T(8,128)(2,1)}, bf16[3,8,128,128]{3,2,1,0:T(8,128)(2,1)}) custom-call(bf16[2,8,128,640]{3,2,1,0:T(8,128)(2,1)S(1)} %get-tuple-element.9.xo, bf16[8,128,512]{2,1,0:T(8,128)(2,1)S(1)} %get-tuple-element.10.wv, f32[8,128,128]{2,1,0:T(8,128)S(1)} %get-tuple-element.11.inv, f32[8,128,640]{2,1,0:T(8,128)S(1)} %get-tuple-element.12.acc, ...), custom_call_target="tpu_custom_call" | custom-call | tf_op jit(solution)/shard_map/last/pallas_call | solution.py:396

commit v5 on v4

--- a/solution.py
+++ b/solution.py
@@ -62,7 +62,7 @@
             device_id={"dom": q}, device_id_type=pl.DeviceIdType.MESH)
 
     def first_copy(h, d):
-        q = dev(g, lax.rem(z + d, NZ), cls)
+        q = dev(g, lax.rem(z + NZ + (1 - 2 * core) * d, NZ), cls)
         return q, remote(hsend.at[h], land.at[h, own_slot], s1.at[h, d], r1.at[h, own_slot], q)
 
     def second_copy(h, d):
@@ -234,12 +234,12 @@
                 right = jnp.concatenate([exts[h][n][cols[k, b]] for k in range(K)], axis=0)
                 acc[b, :, LANES[n]] = jnp.dot(left, right, preferred_element_type=F32)
 
-        if h < HOPS - 1:
-            local_hub = pick(acc)
         for d in FAR_FIRST[::-1]:
             src, landed = arrival(h, d)
             landed.wait_recv()
             third_copy(h, src, core).start()
+        if h < HOPS - 1:
+            local_hub = pick(acc)
 
         @pl.loop(0, NG)
         def _(src):

time: 54.1 us -> 54.1 us (level)
  no operation moved by 1% of the time
where the time goes in v5:
time: 54.1 us; the launch traced here: 54 us
  Pallas kernels  53.4 us (99%)
  between operations  0.64 us (1%)
    pallas_call x1, Pallas kernels, body(): pl.pallas_call(kernel, out_shape=[pltpu.VMEM(*o) for o in outs], in_specs...  51.4 us
    pallas_call x1, Pallas kernels, body(): pl.pallas_call(last, out_shape=(jax.ShapeDtypeStruct((HOPS, BLOCKS, TILE,...  1.99 us

profile of v5, /device:TPU:3, one launch (start us, length us, event | category | flops | bytes accessed | tf_op | source)
XLA Modules:
  0.0 54.0 jit_solution(10504756983340928636)
XLA Ops:
  0.6 51.4 %hops.1 = (bf16[2,8,128,640]{3,2,1,0:T(8,128)(2,1)S(1)}, bf16[8,128,512]{2,1,0:T(8,128)(2,1)S(1)}, f32[8,128,128]{2,1,0:T(8,128)S(1)}, f32[8,128,640]{2,1,0:T(8,128)S(1)}, bf16[16,2,16,640]{3,2,1,0:T(8,128)(2,1)S(1)}) custom-call(bf16[8,128,512]{2,1,0:T(8,128)(2,1)} %bitcast.7, bf16[8,128,128]{2,1,0:T(8,128)(2,1)} %bitcast.9, ...), custom_call_target="tpu_custom_call" | custom-call | tf_op jit(solution)/shard_map/hops/pallas_call | solution.py:356
  52.0 2.0 %last.1 = (bf16[3,8,128,512]{3,2,1,0:T(8,128)(2,1)}, bf16[3,8,128,128]{3,2,1,0:T(8,128)(2,1)}) custom-call(bf16[2,8,128,640]{3,2,1,0:T(8,128)(2,1)S(1)} %get-tuple-element.9.xo, bf16[8,128,512]{2,1,0:T(8,128)(2,1)S(1)} %get-tuple-element.10.wv, f32[8,128,128]{2,1,0:T(8,128)S(1)} %get-tuple-element.11.inv, f32[8,128,640]{2,1,0:T(8,128)S(1)} %get-tuple-element.12.acc, ...), custom_call_target="tpu_custom_call" | custom-call | tf_op jit(solution)/shard_map/last/pallas_call | solution.py:396
